TPU v7x, 128 devices: a whole 4x4x4 slice. The times are simulated.
128 devices in a mesh: seq: 8 (over z_hi, x), exp: 16 (over z_lo, y, core).
Axes of the slice: x: 4, y: 4, z: 4 (z_hi: 2, z_lo: 2; z = z_hi * 2 + z_lo), core: 2. Of those that a mesh axis runs over, the one named last changes fastest.
Arguments:
- queries: bfloat16 [16384, 3072], P(('seq', 'exp')), may hold values from -123 to 123
- keys: bfloat16 [16384, 512], P(('seq', 'exp')), may hold values from -6 to 6
- values: bfloat16 [16384, 512], P(('seq', 'exp')), may hold values from -9 to 9
- residual: bfloat16 [16384, 6144], P(('seq', 'exp')), may hold values from -51 to 51
- proj_weight: bfloat16 [3072, 6144], P('seq', 'exp'), may hold values from -0.109375 to 0.109375
- norm_gain: bfloat16 [6144], replicated, may hold values from 0.099609375 to 1.8984375
- router: bfloat16 [6144, 8], replicated, may hold values from -0.078125 to 0.078125
- expert_ids: int32 [16384, 2], P(('seq', 'exp')), may hold values from 0 to 7, all different within a row; in each aligned block of 128 rows (0 to 127, 128 to 255, ...) at most 33 rows name the same one
- u_gate_up: bfloat16 [16, 3072, 1024], P('exp'), may hold values from -0.078125 to 0.078125
- v_gate_up: bfloat16 [16, 2, 512, 4096], P('exp'), may hold values from -0.25 to 0.25
- u_down: bfloat16 [16, 4096, 512], P('exp'), may hold values from -0.0625 to 0.0625
- v_down: bfloat16 [16, 512, 3072], P('exp'), may hold values from -0.25 to 0.25
Outputs:
- layer_out: bfloat16 [16384, 6144], P(('seq', 'exp'))
Inputs may be any that keep to these rules, and one draw needn't show every extreme that they name: `expert_ids`: the two experts of a token differ. Among the tokens of one device no expert is named more than 33 times, and in some devices' tokens some expert is named exactly 33 times.
All inputs are finite; a program needn't handle non-finite values.
Results may differ from a plain program's by a relative error of at most 0.02.
Values may be sent and summed in bfloat16 or wider, within the bound.
A program may use at most 192 MiB of HBM per device.

v0:
```python
import jax
import jax.numpy as jnp
from jax import lax
from jax.sharding import PartitionSpec as P

D = 6144
HEADS = 24
KV_HEADS = 4
HEAD_DIM = 128
GROUP_HEADS = 3
EXPERTS = 8
RANK = 512
TOK_DEV = 128
CAP = 33
EPS = 1e-05


def in_one_piece(arrays, axis, split_dim, concat_dim, along):
    both = jnp.concatenate(arrays, axis=along)
    out, at, finished = (
        lax.all_to_all(both, axis, split_axis=split_dim, concat_axis=concat_dim, tiled=True),
        0,
        [],
    )
    for a in arrays:
        finished.append(lax.slice_in_dim(out, at, at + a.shape[along], axis=along))
        at += a.shape[along]
    return tuple(finished)


def swapped(x, axis, distance):
    return lax.ppermute(x, axis, [(i, i ^ 1 << distance) for i in range(lax.axis_size(axis))])


def passed_along(value, axis, steps):
    count = lax.axis_size(axis)
    pairs = [(source, (source + steps) % count) for source in range(count)]
    return lax.ppermute(value, axis, pairs)


def attend(current, query_rows, key_rows, value_rows, allowed):
    row_max, row_sum, weighted = current
    scores = jnp.einsum("qhd,kd->qhk", query_rows, key_rows, preferred_element_type=jnp.float32)
    scores = scores * HEAD_DIM ** (-0.5)
    if allowed is not None:
        scores = jnp.where(allowed[:, None, :], scores, -jnp.inf)
    new_max = jnp.maximum(row_max, jnp.max(scores, axis=-1))
    fading = jnp.exp(row_max - new_max)
    exp_terms = jnp.exp(scores - new_max[..., None])
    row_sum = row_sum * fading + jnp.sum(exp_terms, axis=-1)
    update = jnp.einsum(
        "qhk,kd->qhd",
        exp_terms.astype(jnp.bfloat16),
        value_rows,
        preferred_element_type=jnp.float32,
    )
    weighted = weighted * fading[..., None] + update
    return (new_max, row_sum, weighted)


def fresh_states(count_rows):
    query_step = min(512, count_rows)
    states = [
        (
            jnp.full((query_step, GROUP_HEADS), -1e30, jnp.float32),
            jnp.zeros((query_step, GROUP_HEADS), jnp.float32),
            jnp.zeros((query_step, GROUP_HEADS, HEAD_DIM), jnp.float32),
        )
    ]
    return states


def attend_all(states, query_rows, query_pos, key_rows, value_rows, key_pos, mode):
    current = states[0]
    if mode == "open":
        current = attend(current, query_rows, key_rows, value_rows, None)
    else:
        allowed = key_pos[None, :] <= query_pos[:, None]
        current = attend(current, query_rows, key_rows, value_rows, allowed)
    updated = [current]
    return updated


def pick_states(stacked, which):
    return [
        tuple((lax.dynamic_index_in_dim(member, which, 0, keepdims=False) for member in tile))
        for tile in stacked
    ]


def put_states(stacked, which, fresh):
    return [
        tuple(
            (
                lax.dynamic_update_index_in_dim(member, newer, which, 0)
                for member, newer in zip(tile, new_tile)
            )
        )
        for tile, new_tile in zip(stacked, fresh)
    ]


def finish(states):
    results = [weighted / row_sum[..., None] for row_max, row_sum, weighted in states]
    joined = results[0].astype(jnp.bfloat16)
    return joined.reshape(joined.shape[0], GROUP_HEADS * HEAD_DIM)


def per_device(
    queries,
    keys,
    values,
    residual,
    proj_weight,
    norm_gain,
    router,
    expert_ids,
    u_gate_up,
    v_gate_up,
    u_down,
    v_down,
):
    seq_count = lax.axis_size("seq")
    exp_count = lax.axis_size("exp")
    seq_index = lax.axis_index("seq")
    exp_index = lax.axis_index("exp")
    group_count = HEADS // GROUP_HEADS
    split_count = exp_count // group_count
    group_width = GROUP_HEADS * HEAD_DIM
    token_rows = TOK_DEV // split_count
    block_len = TOK_DEV * exp_count
    query_count = exp_count * token_rows
    per_kv = group_count // KV_HEADS
    half_index = exp_index // group_count
    query_send = queries.reshape(token_rows, exp_count, group_width)
    kv_shape = (TOK_DEV, split_count, KV_HEADS, per_kv, HEAD_DIM)
    key_send = jnp.broadcast_to(keys.reshape(TOK_DEV, 1, KV_HEADS, 1, HEAD_DIM), kv_shape).reshape(
        TOK_DEV, exp_count, HEAD_DIM
    )
    value_send = jnp.broadcast_to(
        values.reshape(TOK_DEV, 1, KV_HEADS, 1, HEAD_DIM), kv_shape
    ).reshape(TOK_DEV, exp_count, HEAD_DIM)
    query_got, key_got, value_got = (
        lax.all_to_all(query_send, "exp", split_axis=1, concat_axis=0, tiled=True),
        *in_one_piece((key_send, value_send), "exp", 1, 0, 2),
    )
    query_local = query_got.reshape(query_count, GROUP_HEADS, HEAD_DIM)
    key_local = key_got.reshape(block_len, HEAD_DIM)
    value_local = value_got.reshape(block_len, HEAD_DIM)
    row_ids = jnp.arange(query_count, dtype=jnp.int32)
    in_block = row_ids // token_rows * TOK_DEV + row_ids % token_rows * split_count + half_index
    key_offsets = jnp.arange(block_len, dtype=jnp.int32)
    half_q = query_count // 2
    half_k = block_len // 2
    query_near = query_local[:half_q]
    query_far = query_local[half_q:]
    key_far = key_local[half_k:]
    value_far = value_local[half_k:]
    for bit_index in range(seq_count.bit_length() - 1):
        query_far, key_far, value_far = swapped((query_far, key_far, value_far), "seq", bit_index)
    mirror_index = seq_count - 1 - seq_index
    near_pos = seq_index * block_len + in_block[:half_q]
    far_pos = mirror_index * block_len + in_block[half_q:]
    query_pair = jnp.stack([query_near, query_far])
    pair_states = [
        tuple((jnp.stack([member, member]) for member in tile)) for tile in fresh_states(half_q)
    ]
    held_blocks = (key_local[:half_k], value_local[:half_k], key_far, value_far)
    for step_index in range(seq_count):
        if step_index + 1 < seq_count:
            arrived = passed_along(
                (held_blocks[0], held_blocks[1], held_blocks[2], held_blocks[3]), "seq", 1
            )
        source = (seq_index - step_index) % seq_count
        low_keys, low_values, high_keys, high_values = held_blocks
        if step_index == 0:
            low_pos = source * block_len + key_offsets[:half_k]
            high_pos = (seq_count - 1 - source) * block_len + half_k + key_offsets[:half_k]
            near_now = pick_states(pair_states, 0)
            near_now = attend_all(
                near_now, query_near, near_pos, low_keys, low_values, low_pos, "masked"
            )
            pair_states = put_states(pair_states, 0, near_now)
            far_now = pick_states(pair_states, 1)
            far_now = attend_all(
                far_now, query_far, far_pos, high_keys, high_values, high_pos, "masked"
            )
            pair_states = put_states(pair_states, 1, far_now)
        else:
            first_low = source <= seq_index
            first_slot = jnp.where(first_low, 0, 1).astype(jnp.int32)
            key_pick = jnp.where(first_low, low_keys, high_keys)
            value_pick = jnp.where(first_low, low_values, high_values)
            query_pick = lax.dynamic_index_in_dim(query_pair, first_slot, 0, keepdims=False)
            picked_states = attend_all(
                pick_states(pair_states, first_slot),
                query_pick,
                None,
                key_pick,
                value_pick,
                None,
                "open",
            )
            pair_states = put_states(pair_states, first_slot, picked_states)
        second_high = source >= seq_count - seq_index
        second_slot = jnp.where(second_high, 0, 1).astype(jnp.int32)
        key_pick = jnp.where(second_high, high_keys, low_keys)
        value_pick = jnp.where(second_high, high_values, low_values)
        query_pick = lax.dynamic_index_in_dim(query_pair, second_slot, 0, keepdims=False)
        picked_states = attend_all(
            pick_states(pair_states, second_slot),
            query_pick,
            None,
            key_pick,
            value_pick,
            None,
            "open",
        )
        pair_states = put_states(pair_states, second_slot, picked_states)
        if step_index + 1 < seq_count:
            held_blocks = arrived
    attended_near = finish(pick_states(pair_states, 0))
    attended_far = finish(pick_states(pair_states, 1))
    for bit_index in range(seq_count.bit_length() - 1):
        attended_far = swapped(attended_far, "seq", bit_index)
    attended = jnp.concatenate([attended_near, attended_far], axis=0)
    weight_rows = lax.all_gather(proj_weight, "seq", axis=0, tiled=True)
    column_count = weight_rows.shape[1]
    blank_sum = jnp.zeros((exp_count, token_rows, split_count, column_count), jnp.float32)
    carried = blank_sum
    shard_piece = lax.all_gather(attended, "exp", axis=0, tiled=True)
    start_row = jnp.int32(0)
    shard_total = shard_piece.shape[0] // query_count
    for shard_index in range(shard_total):
        device_id = start_row // query_count + shard_index
        group_id = device_id % group_count
        half_id = device_id // group_count
        weight_slice = lax.dynamic_slice_in_dim(weight_rows, group_id * group_width, group_width, 0)
        rows_now = shard_piece[shard_index * query_count : (shard_index + 1) * query_count]
        product = jnp.dot(rows_now, weight_slice, preferred_element_type=jnp.float32)
        product = product.reshape(exp_count, token_rows, 1, column_count)
        corner = (0, 0, half_id, 0)
        present = lax.dynamic_slice(carried, corner, (exp_count, token_rows, 1, column_count))
        carried = lax.dynamic_update_slice(carried, present + product, corner)
    projected = carried
    projected = projected.reshape(block_len, column_count)
    attn_block = projected.astype(jnp.bfloat16)
    attn_update = lax.all_to_all(attn_block, "exp", split_axis=0, concat_axis=1, tiled=True)
    stream = residual.astype(jnp.float32) + attn_update.astype(jnp.float32)
    mean_sq = jnp.mean(stream * stream, axis=-1, keepdims=True)
    normed = (stream * lax.rsqrt(mean_sq + EPS) * norm_gain.astype(jnp.float32)).astype(
        jnp.bfloat16
    )
    logits = jnp.dot(normed, router, preferred_element_type=jnp.float32)
    expert_range = jnp.arange(EXPERTS, dtype=jnp.int32)
    picked = (expert_ids[:, :, None] == expert_range[None, None, :]).astype(jnp.float32)
    chosen = jnp.sum(picked * logits[:, None, :], axis=-1)
    mix_first = jax.nn.sigmoid(chosen[:, 0] - chosen[:, 1])
    mix_second = jax.nn.sigmoid(chosen[:, 1] - chosen[:, 0])
    piece_count = exp_count // EXPERTS
    piece_width = D // piece_count
    flat_ids = expert_ids.reshape(TOK_DEV * 2)
    member = (flat_ids[:, None] == expert_range[None, :]).astype(jnp.int32)
    slot_of = jnp.sum((jnp.cumsum(member, axis=0) - 1) * member, axis=1)
    token_of = jnp.arange(TOK_DEV * 2, dtype=jnp.int32) // 2
    slot_range = jnp.arange(CAP, dtype=jnp.int32)
    filled = member[:, :, None] * (slot_of[:, None, None] == slot_range[None, None, :]).astype(
        jnp.int32
    )
    source_token = jnp.sum(filled * token_of[:, None, None], axis=0)
    occupied = jnp.sum(filled, axis=0)
    piece_range = jnp.arange(piece_count, dtype=jnp.int32)
    take_index = source_token[:, None, :] * piece_count + piece_range[None, :, None]
    normed_rows = normed.reshape(TOK_DEV * piece_count, piece_width)
    send_rows = jnp.take(normed_rows, take_index, axis=0) * occupied[:, None, :, None].astype(
        jnp.bfloat16
    )
    send_rows = send_rows.reshape(exp_count, CAP, piece_width)
    dispatched = lax.all_to_all(send_rows, "exp", split_axis=0, concat_axis=0, tiled=True)
    expert_rows = dispatched.reshape(exp_count * CAP, piece_width)
    rank_sum = jnp.dot(expert_rows, u_gate_up[0], preferred_element_type=jnp.float32)
    bit_index = 0
    rank_sum = rank_sum + swapped(rank_sum.astype(jnp.bfloat16), "exp", bit_index).astype(
        rank_sum.dtype
    )
    rank_in = rank_sum.astype(jnp.bfloat16)
    gate_part = jnp.dot(rank_in[:, :RANK], v_gate_up[0, 0], preferred_element_type=jnp.float32)
    up_part = jnp.dot(rank_in[:, RANK:], v_gate_up[0, 1], preferred_element_type=jnp.float32)
    hidden = (jax.nn.silu(gate_part) * up_part).astype(jnp.bfloat16)
    down_sum = jnp.dot(hidden, u_down[0], preferred_element_type=jnp.float32)
    bit_index = 0
    down_sum = down_sum + swapped(down_sum.astype(jnp.bfloat16), "exp", bit_index).astype(
        down_sum.dtype
    )
    expert_out = jnp.dot(
        down_sum.astype(jnp.bfloat16), v_down[0], preferred_element_type=jnp.float32
    ).astype(jnp.bfloat16)
    returned = lax.all_to_all(
        expert_out.reshape(exp_count, CAP, piece_width),
        "exp",
        split_axis=0,
        concat_axis=0,
        tiled=True,
    )
    returned_rows = returned.reshape(exp_count * CAP, piece_width)
    slot_pairs = slot_of.reshape(TOK_DEV, 2)
    fetch_index = (
        expert_ids[:, :, None] * piece_count + piece_range[None, None, :]
    ) * CAP + slot_pairs[:, :, None]
    fetched = jnp.take(returned_rows, fetch_index, axis=0).astype(jnp.float32)
    fetched = fetched.reshape(TOK_DEV, 2, D)
    mixture = mix_first[:, None] * fetched[:, 0] + mix_second[:, None] * fetched[:, 1]
    return (stream + mixture).astype(jnp.bfloat16)


def solution(mesh):
    in_specs = (
        P(("seq", "exp"), None),
        P(("seq", "exp"), None),
        P(("seq", "exp"), None),
        P(("seq", "exp"), None),
        P("seq", "exp"),
        P(),
        P(),
        P(("seq", "exp"), None),
        P("exp", None, None),
        P("exp", None, None, None),
        P("exp", None, None),
        P("exp", None, None),
    )
    out_specs = P(("seq", "exp"), None)
    return jax.shard_map(
        per_device, mesh=mesh, in_specs=in_specs, out_specs=out_specs, check_vma=False
    )
```

profile of v0, /device:TPU:8, one launch (start us, length us, event | category | flops | bytes accessed | tf_op | source)
XLA Modules:
  0.0 711.7 jit_solution(16518140641565439048)
XLA Ops:
  19.6 8.3 %all-to-all-done.1 = bf16[64,16,384]{2,0,1:T(8,128)(2,1)} async-done(((bf16[64,16,384]{2,0,1:T(8,128)(2,1)}), bf16[64,16,384]{2,0,1:T(8,128)(2,1)}, u32[]{:S(2)}, u32[]{:S(2)}) %all-to-all-start.1) | async-done | bytes 786464 | tf_op jit(solution)/shard_map/all_to_all | solution.py:144
  27.9 7.4 %all-to-all-start = ((bf16[128,16,256]{2,0,1:T(8,128)(2,1)}), bf16[128,16,256]{2,0,1:T(8,128)(2,1)}, u32[]{:S(2)}, u32[]{:S(2)}) async-start(bf16[128,16,256]{2,0,1:T(8,128)(2,1)} %pad_maximum_fusion.1), calls=%async_computation | async-start | bytes 2097152 | tf_op jit(solution)/shard_map/all_to_all | solution.py:21
  80.9 6.5 collective-permute-done.11
  92.5 13.6 %collective-permute-done.1 = bf16[1024,128]{1,0:T(8,128)(2,1)S(1)} collective-permute-done((bf16[1024,128]{1,0:T(8,128)(2,1)S(1)}, bf16[1024,128]{1,0:T(8,128)(2,1)S(1)}, u32[]{:S(2)}, u32[]{:S(2)}) %collective-permute-start.1) | collective-permute-done | bytes 262176 | tf_op jit(solution)/shard_map/ppermute | solution.py:32
  127.3 8.9 %collective-permute-done.2 = bf16[1024,128]{1,0:T(8,128)(2,1)S(1)} collective-permute-done((bf16[1024,128]{1,0:T(8,128)(2,1)S(1)}, bf16[1024,128]{1,0:T(8,128)(2,1)S(1)}, u32[]{:S(2)}, u32[]{:S(2)}) %collective-permute-start.2) | collective-permute-done | bytes 262176 | tf_op jit(solution)/shard_map/ppermute | solution.py:32
  144.3 24.7 %collective-permute-done.5 = bf16[512,3,128]{2,0,1:T(8,128)(2,1)S(1)} collective-permute-done((bf16[512,3,128]{2,0,1:T(8,128)(2,1)S(1)}, bf16[512,3,128]{2,0,1:T(8,128)(2,1)S(1)}, u32[]{:S(2)}, u32[]{:S(2)}) %collective-permute-start.5) | collective-permute-done | bytes 393248 | tf_op jit(solution)/shard_map/ppermute | solution.py:32
  188.5 7.0 collective-permute-start.27
  255.6 11.0 %collective-permute-done.26 = bf16[1024,128]{1,0:T(8,128)(2,1)S(1)} collective-permute-done((bf16[1024,128]{1,0:T(8,128)(2,1)S(1)}, bf16[1024,128]{1,0:T(8,128)(2,1)S(1)}, u32[]{:S(2)}, u32[]{:S(2)}) %collective-permute-start.26) | collective-permute-done | bytes 262176 | tf_op jit(solution)/shard_map/ppermute | solution.py:38
  276.8 10.7 %collective-permute-done.30 = bf16[1024,128]{1,0:T(8,128)(2,1)S(1)} collective-permute-done((bf16[1024,128]{1,0:T(8,128)(2,1)S(1)}, bf16[1024,128]{1,0:T(8,128)(2,1)S(1)}, u32[]{:S(2)}, u32[]{:S(2)}) %collective-permute-start.30) | collective-permute-done | bytes 262176 | tf_op jit(solution)/shard_map/ppermute | solution.py:38
  296.5 10.5 %collective-permute-done.34 = bf16[1024,128]{1,0:T(8,128)(2,1)S(1)} collective-permute-done((bf16[1024,128]{1,0:T(8,128)(2,1)S(1)}, bf16[1024,128]{1,0:T(8,128)(2,1)S(1)}, u32[]{:S(2)}, u32[]{:S(2)}) %collective-permute-start.34) | collective-permute-done | bytes 262176 | tf_op jit(solution)/shard_map/ppermute | solution.py:38
  316.9 10.4 %collective-permute-done.37 = bf16[512,384]{0,1:T(8,128)(2,1)S(1)} collective-permute-done((bf16[512,384]{0,1:T(8,128)(2,1)S(1)}, bf16[512,384]{0,1:T(8,128)(2,1)S(1)}, u32[]{:S(2)}, u32[]{:S(2)}) %collective-permute-start.37) | collective-permute-done | bytes 393248 | tf_op jit(solution)/shard_map/ppermute | solution.py:32
  327.4 9.3 %collective-permute-done.38 = bf16[512,384]{0,1:T(8,128)(2,1)S(1)} collective-permute-done((bf16[512,384]{0,1:T(8,128)(2,1)S(1)}, bf16[512,384]{0,1:T(8,128)(2,1)S(1)}, u32[]{:S(2)}, u32[]{:S(2)}) %collective-permute-start.38) | collective-permute-done | bytes 393248 | tf_op jit(solution)/shard_map/ppermute | solution.py:32
  336.7 9.2 %collective-permute-done.39 = bf16[512,384]{0,1:T(8,128)(2,1)S(1)} collective-permute-done((bf16[512,384]{0,1:T(8,128)(2,1)S(1)}, bf16[512,384]{0,1:T(8,128)(2,1)S(1)}, u32[]{:S(2)}, u32[]{:S(2)}) %collective-permute-start.39) | collective-permute-done | bytes 393248 | tf_op jit(solution)/shard_map/ppermute | solution.py:32
  348.2 66.8 %all-gather.3.cloned.1.call-done = bf16[16384,384]{0,1:T(8,128)(2,1)} async-done(((bf16[1024,384]{0,1:T(8,128)(2,1)}), bf16[16384,384]{0,1:T(8,128)(2,1)}) %all-gather.3.cloned.1.call-update) | async-done | bytes 12582928 | tf_op jit(solution)/shard_map/all_gather | solution.py:231
  469.9 16.8 %all-to-all-done.2 = bf16[16,128,384]{2,1,0:T(8,128)(2,1)} async-done(((bf16[16,128,384]{2,1,0:T(8,128)(2,1)}), bf16[16,128,384]{2,1,0:T(8,128)(2,1)}, u32[]{:S(2)}, u32[]{:S(2)}) %all-to-all-start.2) | async-done | bytes 1572896 | tf_op jit(solution)/shard_map/all_to_all | solution.py:248
  500.2 10.8 %gather_fusion = bf16[528,3072]{1,0:T(8,128)(2,1)} fusion(bf16[256,3072]{1,0:T(8,128)(2,1)} %reshape.799, s32[1024]{0:T(1024)S(1)} %pad_clamp_fusion.1), kind=kCustom, calls=%fused_computation | custom fusion | bytes 6490176 | tf_op jit(solution)/shard_map/jit(_take)/gather | solution.py:275
  517.4 49.3 %all_to_all.53 = bf16[16,33,3072]{2,1,0:T(8,128)(2,1)} all-to-all(bf16[16,33,3072]{2,1,0:T(8,128)(2,1)S(1)} %select_multiply_fusion), channel_id=1, replica_groups=mesh['seq'=8,'exp'=16] {'exp'}, dimensions={0} | all-to-all | bytes 6488064 | tf_op jit(solution)/shard_map/all_to_all | solution.py:279
  570.6 6.6 fusion.607
  602.9 6.8 all-to-all-start.4
  612.3 50.5 %all-to-all-done.4 = bf16[16,33,3072]{2,1,0:T(8,128)(2,1)} async-done(((bf16[16,33,3072]{2,1,0:T(8,128)(2,1)}), bf16[16,33,3072]{2,1,0:T(8,128)(2,1)}, u32[]{:S(2)}, u32[]{:S(2)}) %all-to-all-start.4) | async-done | bytes 3244064 | tf_op jit(solution)/shard_map/all_to_all | solution.py:298
  666.7 9.4 %gather_fusion.1 = bf16[512,3072]{1,0:T(8,128)(2,1)} fusion(bf16[528,3072]{1,0:T(8,128)(2,1)} %reshape.802, s32[1024]{0:T(1024)S(1)} %pad_clamp_fusion), kind=kCustom, calls=%fused_computation.1 | custom fusion | bytes 6293504 | tf_op jit(solution)/shard_map/jit(_take)/gather | solution.py:310
  676.1 7.2 %reshape.814 = bf16[128,2,2,3072]{3,2,1,0:T(2,128)(2,1)} reshape(bf16[512,3072]{1,0:T(8,128)(2,1)} %gather_fusion.1) | data formatting | bytes 6291456 | tf_op jit(solution)/shard_map/jit(_take)/gather | solution.py:310
  683.3 6.6 fusion.81
  689.9 6.6 copy.356
  (326 shorter events, 321.8 us)
Async XLA Ops:
  17.4 330.9 %all-gather.5.cloned.1.call-start = ((), (), s32[]{:S(2)}) async-start(), calls=%async_computation.6 | async-start | bytes 2654208 | tf_op jit(solution)/shard_map/all_gather | solution.py:227
  35.3 379.7 %all-gather.3.cloned.1.call-start = ((), (), s32[]{:S(2)}) async-start(), calls=%async_computation.5 | async-start | bytes 13369344 | tf_op jit(solution)/shard_map/all_gather | solution.py:231
  52.1 24.0 %collective-permute-start.6 = (bf16[1024,128]{1,0:T(8,128)(2,1)S(1)}, bf16[1024,128]{1,0:T(8,128)(2,1)S(1)}, u32[]{:S(2)}, u32[]{:S(2)}) collective-permute-start(bf16[1024,128]{1,0:T(8,128)(2,1)S(1)} %get-tuple-element.48), channel_id=1, source_target_pairs={{0,16},{16,0},{32,48},{48,32},{64,80},{80,64},{96,112},{112,96},{1... | collective-permute-start | bytes 786440 | tf_op jit(solution)/shard_map/ppermute | solution.py:32
  52.6 26.9 %collective-permute-start.9 = (bf16[1024,128]{1,0:T(8,128)(2,1)S(1)}, bf16[1024,128]{1,0:T(8,128)(2,1)S(1)}, u32[]{:S(2)}, u32[]{:S(2)}) collective-permute-start(bf16[1024,128]{1,0:T(8,128)(2,1)S(1)} %get-tuple-element.50), channel_id=1, source_target_pairs={{0,16},{16,32},{32,48},{48,64},{64,80},{80,96},{96,112},{112,0},{1... | collective-permute-start | bytes 786440 | tf_op jit(solution)/shard_map/ppermute | solution.py:38
  54.1 33.3 %collective-permute-start.11 = (bf16[1024,128]{1,0:T(8,128)(2,1)S(1)}, bf16[1024,128]{1,0:T(8,128)(2,1)S(1)}, u32[]{:S(2)}, u32[]{:S(2)}) collective-permute-start(bf16[1024,128]{1,0:T(8,128)(2,1)S(1)} %get-tuple-element.47), channel_id=1, source_target_pairs={{0,16},{16,32},{32,48},{48,64},{64,80},{80,96},{96,112},{112,0},{1... | collective-permute-start | bytes 786440 | tf_op jit(solution)/shard_map/ppermute | solution.py:38
  59.7 62.4 %collective-permute-start.4 = (bf16[512,3,128]{2,0,1:T(8,128)(2,1)}, bf16[512,3,128]{2,0,1:T(8,128)(2,1)S(1)}, u32[]{:S(2)}, u32[]{:S(2)}) collective-permute-start(bf16[512,3,128]{2,0,1:T(8,128)(2,1)} %collective-permute-done.3), channel_id=1, source_target_pairs={{0,32},{16,48},{32,0},{48,16},{64,96},{80,112},{96,64},{112,80},{1... | collective-permute-start | bytes 1179656 | tf_op jit(solution)/shard_map/ppermute | solution.py:32
  67.8 38.2 %collective-permute-start.1 = (bf16[1024,128]{1,0:T(8,128)(2,1)S(1)}, bf16[1024,128]{1,0:T(8,128)(2,1)S(1)}, u32[]{:S(2)}, u32[]{:S(2)}) collective-permute-start(bf16[1024,128]{1,0:T(8,128)(2,1)S(1)} %collective-permute-done), channel_id=1, source_target_pairs={{0,32},{16,48},{32,0},{48,16},{64,96},{80,112},{96,64},{112,80},{1... | collective-permute-start | bytes 786440 | tf_op jit(solution)/shard_map/ppermute | solution.py:32
  76.0 35.6 %collective-permute-start.7 = (bf16[1024,128]{1,0:T(8,128)(2,1)S(1)}, bf16[1024,128]{1,0:T(8,128)(2,1)S(1)}, u32[]{:S(2)}, u32[]{:S(2)}) collective-permute-start(bf16[1024,128]{1,0:T(8,128)(2,1)S(1)} %collective-permute-done.6), channel_id=1, source_target_pairs={{0,32},{16,48},{32,0},{48,16},{64,96},{80,112},{96,64},{112,80},{1... | collective-permute-start | bytes 786440 | tf_op jit(solution)/shard_map/ppermute | solution.py:32
  79.5 36.8 %collective-permute-start.13 = (bf16[1024,128]{1,0:T(8,128)(2,1)S(1)}, bf16[1024,128]{1,0:T(8,128)(2,1)S(1)}, u32[]{:S(2)}, u32[]{:S(2)}) collective-permute-start(bf16[1024,128]{1,0:T(8,128)(2,1)S(1)} %collective-permute-done.9), channel_id=1, source_target_pairs={{0,16},{16,32},{32,48},{48,64},{64,80},{80,96},{96,112},{112,0},{1... | collective-permute-start | bytes 786440 | tf_op jit(solution)/shard_map/ppermute | solution.py:38
  87.4 33.8 %collective-permute-start.15 = (bf16[1024,128]{1,0:T(8,128)(2,1)S(1)}, bf16[1024,128]{1,0:T(8,128)(2,1)S(1)}, u32[]{:S(2)}, u32[]{:S(2)}) collective-permute-start(bf16[1024,128]{1,0:T(8,128)(2,1)S(1)} %collective-permute-done.11), channel_id=1, source_target_pairs={{0,16},{16,32},{32,48},{48,64},{64,80},{80,96},{96,112},{112,0},{1... | collective-permute-start | bytes 786440 | tf_op jit(solution)/shard_map/ppermute | solution.py:38
  106.1 30.1 %collective-permute-start.2 = (bf16[1024,128]{1,0:T(8,128)(2,1)S(1)}, bf16[1024,128]{1,0:T(8,128)(2,1)S(1)}, u32[]{:S(2)}, u32[]{:S(2)}) collective-permute-start(bf16[1024,128]{1,0:T(8,128)(2,1)S(1)} %collective-permute-done.1), channel_id=1, source_target_pairs={{0,64},{16,80},{32,96},{48,112},{64,0},{80,16},{96,32},{112,48},{1... | collective-permute-start | bytes 786440 | tf_op jit(solution)/shard_map/ppermute | solution.py:32
  111.6 30.2 %collective-permute-start.8 = (bf16[1024,128]{1,0:T(8,128)(2,1)S(1)}, bf16[1024,128]{1,0:T(8,128)(2,1)S(1)}, u32[]{:S(2)}, u32[]{:S(2)}) collective-permute-start(bf16[1024,128]{1,0:T(8,128)(2,1)S(1)} %collective-permute-done.7), channel_id=1, source_target_pairs={{0,64},{16,80},{32,96},{48,112},{64,0},{80,16},{96,32},{112,48},{1... | collective-permute-start | bytes 786440 | tf_op jit(solution)/shard_map/ppermute | solution.py:32
  116.2 25.6 %collective-permute-start.17 = (bf16[1024,128]{1,0:T(8,128)(2,1)S(1)}, bf16[1024,128]{1,0:T(8,128)(2,1)S(1)}, u32[]{:S(2)}, u32[]{:S(2)}) collective-permute-start(bf16[1024,128]{1,0:T(8,128)(2,1)S(1)} %collective-permute-done.13), channel_id=1, source_target_pairs={{0,16},{16,32},{32,48},{48,64},{64,80},{80,96},{96,112},{112,0},{1... | collective-permute-start | bytes 786440 | tf_op jit(solution)/shard_map/ppermute | solution.py:38
  122.1 46.8 %collective-permute-start.5 = (bf16[512,3,128]{2,0,1:T(8,128)(2,1)S(1)}, bf16[512,3,128]{2,0,1:T(8,128)(2,1)S(1)}, u32[]{:S(2)}, u32[]{:S(2)}) collective-permute-start(bf16[512,3,128]{2,0,1:T(8,128)(2,1)S(1)} %collective-permute-done.4), channel_id=1, source_target_pairs={{0,64},{16,80},{32,96},{48,112},{64,0},{80,16},{96,32},{112,48},{1... | collective-permute-start | bytes 1179656 | tf_op jit(solution)/shard_map/ppermute | solution.py:32
  136.2 43.8 %collective-permute-start.10 = (bf16[1024,128]{1,0:T(8,128)(2,1)S(1)}, bf16[1024,128]{1,0:T(8,128)(2,1)S(1)}, u32[]{:S(2)}, u32[]{:S(2)}) collective-permute-start(bf16[1024,128]{1,0:T(8,128)(2,1)S(1)} %collective-permute-done.2), channel_id=1, source_target_pairs={{0,16},{16,32},{32,48},{48,64},{64,80},{80,96},{96,112},{112,0},{1... | collective-permute-start | bytes 786440 | tf_op jit(solution)/shard_map/ppermute | solution.py:38
  141.8 40.6 %collective-permute-start.12 = (bf16[1024,128]{1,0:T(8,128)(2,1)S(1)}, bf16[1024,128]{1,0:T(8,128)(2,1)S(1)}, u32[]{:S(2)}, u32[]{:S(2)}) collective-permute-start(bf16[1024,128]{1,0:T(8,128)(2,1)S(1)} %collective-permute-done.8), channel_id=1, source_target_pairs={{0,16},{16,32},{32,48},{48,64},{64,80},{80,96},{96,112},{112,0},{1... | collective-permute-start | bytes 786440 | tf_op jit(solution)/shard_map/ppermute | solution.py:38
  141.8 46.2 %collective-permute-start.21 = (bf16[1024,128]{1,0:T(8,128)(2,1)S(1)}, bf16[1024,128]{1,0:T(8,128)(2,1)S(1)}, u32[]{:S(2)}, u32[]{:S(2)}) collective-permute-start(bf16[1024,128]{1,0:T(8,128)(2,1)S(1)} %collective-permute-done.17), channel_id=1, source_target_pairs={{0,16},{16,32},{32,48},{48,64},{64,80},{80,96},{96,112},{112,0},{1... | collective-permute-start | bytes 786440 | tf_op jit(solution)/shard_map/ppermute | solution.py:38
  141.8 46.7 %collective-permute-start.23 = (bf16[1024,128]{1,0:T(8,128)(2,1)S(1)}, bf16[1024,128]{1,0:T(8,128)(2,1)S(1)}, u32[]{:S(2)}, u32[]{:S(2)}) collective-permute-start(bf16[1024,128]{1,0:T(8,128)(2,1)S(1)} %collective-permute-done.19), channel_id=1, source_target_pairs={{0,16},{16,32},{32,48},{48,64},{64,80},{80,96},{96,112},{112,0},{1... | collective-permute-start | bytes 786440 | tf_op jit(solution)/shard_map/ppermute | solution.py:38
  188.5 27.5 %collective-permute-start.27 = (bf16[1024,128]{1,0:T(8,128)(2,1)S(1)}, bf16[1024,128]{1,0:T(8,128)(2,1)S(1)}, u32[]{:S(2)}, u32[]{:S(2)}) collective-permute-start(bf16[1024,128]{1,0:T(8,128)(2,1)S(1)} %collective-permute-done.23), channel_id=1, source_target_pairs={{0,16},{16,32},{32,48},{48,64},{64,80},{80,96},{96,112},{112,0},{1... | collective-permute-start | bytes 786440 | tf_op jit(solution)/shard_map/ppermute | solution.py:38
  210.4 22.5 %collective-permute-start.29 = (bf16[1024,128]{1,0:T(8,128)(2,1)S(1)}, bf16[1024,128]{1,0:T(8,128)(2,1)S(1)}, u32[]{:S(2)}, u32[]{:S(2)}) collective-permute-start(bf16[1024,128]{1,0:T(8,128)(2,1)S(1)} %collective-permute-done.25), channel_id=1, source_target_pairs={{0,16},{16,32},{32,48},{48,64},{64,80},{80,96},{96,112},{112,0},{1... | collective-permute-start | bytes 786440 | tf_op jit(solution)/shard_map/ppermute | solution.py:38
  232.9 63.5 %collective-permute-start.33 = (bf16[1024,128]{1,0:T(8,128)(2,1)S(1)}, bf16[1024,128]{1,0:T(8,128)(2,1)S(1)}, u32[]{:S(2)}, u32[]{:S(2)}) collective-permute-start(bf16[1024,128]{1,0:T(8,128)(2,1)S(1)} %collective-permute-done.29), channel_id=1, source_target_pairs={{0,16},{16,32},{32,48},{48,64},{64,80},{80,96},{96,112},{112,0},{1... | collective-permute-start | bytes 786440 | tf_op jit(solution)/shard_map/ppermute | solution.py:38
  238.5 69.6 %collective-permute-start.35 = (bf16[1024,128]{1,0:T(8,128)(2,1)S(1)}, bf16[1024,128]{1,0:T(8,128)(2,1)S(1)}, u32[]{:S(2)}, u32[]{:S(2)}) collective-permute-start(bf16[1024,128]{1,0:T(8,128)(2,1)S(1)} %collective-permute-done.31), channel_id=1, source_target_pairs={{0,16},{16,32},{32,48},{48,64},{64,80},{80,96},{96,112},{112,0},{1... | collective-permute-start | bytes 786440 | tf_op jit(solution)/shard_map/ppermute | solution.py:38
  459.7 26.9 %all-to-all-start.2 = ((bf16[16,128,384]{2,1,0:T(8,128)(2,1)}), bf16[16,128,384]{2,1,0:T(8,128)(2,1)}, u32[]{:S(2)}, u32[]{:S(2)}) async-start(bf16[16,128,384]{2,1,0:T(8,128)(2,1)} %copy.346), calls=%async_computation.2 | async-start | bytes 3145728 | tf_op jit(solution)/shard_map/all_to_all | solution.py:248
  602.9 60.0 %all-to-all-start.4 = ((bf16[16,33,3072]{2,1,0:T(8,128)(2,1)}), bf16[16,33,3072]{2,1,0:T(8,128)(2,1)}, u32[]{:S(2)}, u32[]{:S(2)}) async-start(bf16[16,33,3072]{2,1,0:T(8,128)(2,1)} %reshape.801), calls=%async_computation.4 | async-start | bytes 7864320 | tf_op jit(solution)/shard_map/all_to_all | solution.py:298
  (37 other events, 1130.7 us)
Sparse Core Ops, SparseCore 0:
  20.5 90.7 all-gather.4
  347.0 67.9 all-gather.2
where the time goes:
time: 721 us; the launch traced here: 712 us
  waiting for transfers between devices  322 us (45%)
  matrix products  87 us (12%)
  local copies, waits for them, and re-layouts  83.5 us (12%)
  other arithmetic  77.6 us (11%)
  starting transfers between devices  76.9 us (11%)
  blocking collectives  49.3 us (7%)
  between operations  15.1 us (2%)
    ppermute x14, waiting for transfers between devices, swapped(): lax.ppermute(x, axis, [(i, i ^ 1 << distance) for i in range(lax.axis_siz...  98.9 us
    ppermute x28, waiting for transfers between devices, passed_along(): return lax.ppermute(value, axis, pairs)  79.1 us
    all_gather x1, waiting for transfers between devices, per_device(): shard_piece = lax.all_gather(attended, 'exp', axis=0, tiled=True)  66.8 us
    all_to_all x1, waiting for transfers between devices, per_device(): lax.all_to_all(expert_out.reshape(exp_count, CAP, piece_width), 'exp', sp...  50.5 us
    all_to_all x1, blocking collectives, per_device(): lax.all_to_all(send_rows, 'exp', split_axis=0, concat_axis=0, tiled=True)  49.3 us
    dot_general x17, matrix products, attend(): jnp.einsum('qhk,kd->qhd', exp_terms.astype(jnp.bfloat16), value_rows, pre...  27 us
    dynamic_update_slice x15, other arithmetic, per_device(): carried = lax.dynamic_update_slice(carried, present + product, corner)  26.5 us
    ppermute x14, starting transfers between devices, swapped(): lax.ppermute(x, axis, [(i, i ^ 1 << distance) for i in range(lax.axis_siz...  26 us
  transfers between devices with their start and end apart: 48, of which 35 were waited for; matrix products, arithmetic and copies ran while one was open for 13% of the time, Pallas kernels for 0%

commit v1 on v0

--- a/solution.py
+++ b/solution.py
@@ -228,7 +228,9 @@
     column_count = weight_rows.shape[1]
     blank_sum = jnp.zeros((exp_count, token_rows, split_count, column_count), jnp.float32)
     carried = blank_sum
-    shard_piece = lax.all_gather(attended, "exp", axis=0, tiled=True)
+    shard_piece = jnp.concatenate(
+        lax.all_to_all(jnp.stack([attended] * lax.axis_size("exp")), "exp", 0, 0), axis=0
+    )
     start_row = jnp.int32(0)
     shard_total = shard_piece.shape[0] // query_count
     for shard_index in range(shard_total):

time: 721 us -> 813 us (1.13)
  waiting for transfers between devices: 322 us -> 393 us
  other arithmetic: 77.6 us -> 50.9 us
  local copies, waits for them, and re-layouts: 83.5 us -> 103 us
  starting transfers between devices: 76.9 us -> 92.8 us
  matrix products: 87 us -> 99.6 us
    all_to_all x0 -> x1, waiting for transfers between devices: none -> 168 us  [per_device(): lax.all_to_all(jnp.stack([attended] * lax.axis_size('exp')), 'exp', 0, 0)]
    all_gather x1 -> x0, waiting for transfers between devices: 66.8 us -> none  [per_device(): shard_piece = lax.all_gather(attended, 'exp', axis=0, tiled=True)]
    dynamic_update_slice x15 -> x0, other arithmetic: 26.5 us -> none  [per_device(): carried = lax.dynamic_update_slice(carried, present + product, corner)]
    ppermute x14, waiting for transfers between devices: 98.9 us -> 81.8 us  [swapped(): lax.ppermute(x, axis, [(i, i ^ 1 << distance) for i in range(lax.axis_siz...]
    ppermute x28, waiting for transfers between devices: 79.1 us -> 66 us  [passed_along(): return lax.ppermute(value, axis, pairs)]
    dot_general x16, matrix products: 14.7 us -> 27.1 us  [per_device(): jnp.dot(rows_now, weight_slice, preferred_element_type=jnp.float32)]
    slice x1 -> x2, local copies, waits for them, and re-layouts: 0.21 us -> 9.95 us  [the longest x1 9.74 us: per_device(): shard_piece[shard_index * query_count:(shard_index + 1) * query_count]]
  transfers between devices with their start and end apart: 48 -> 48, of which waited for: 35 -> 36; matrix products, arithmetic and copies ran while one was open for 13% -> 12% of each run, Pallas kernels for 0% -> 0%
where the time goes in v1:
time: 813 us; the launch traced here: 803 us
  waiting for transfers between devices  393 us (48%)
  local copies, waits for them, and re-layouts  103 us (13%)
  matrix products  99.6 us (12%)
  starting transfers between devices  92.8 us (11%)
  other arithmetic  50.9 us (6%)
  blocking collectives  49 us (6%)
  between operations  15.5 us (2%)
    all_to_all x1, waiting for transfers between devices, per_device(): lax.all_to_all(jnp.stack([attended] * lax.axis_size('exp')), 'exp', 0, 0)  168 us
    ppermute x14, waiting for transfers between devices, swapped(): lax.ppermute(x, axis, [(i, i ^ 1 << distance) for i in range(lax.axis_siz...  81.8 us
    ppermute x28, waiting for transfers between devices, passed_along(): return lax.ppermute(value, axis, pairs)  66 us
    all_to_all x1, waiting for transfers between devices, per_device(): lax.all_to_all(expert_out.reshape(exp_count, CAP, piece_width), 'exp', sp...  50.5 us
    all_to_all x1, blocking collectives, per_device(): lax.all_to_all(send_rows, 'exp', split_axis=0, concat_axis=0, tiled=True)  49 us
    ppermute x14, starting transfers between devices, swapped(): lax.ppermute(x, axis, [(i, i ^ 1 << distance) for i in range(lax.axis_siz...  31.8 us
    ppermute x28, starting transfers between devices, passed_along(): return lax.ppermute(value, axis, pairs)  30.3 us
    dot_general x17, matrix products, attend(): jnp.einsum('qhk,kd->qhd', exp_terms.astype(jnp.bfloat16), value_rows, pre...  27.2 us
  transfers between devices with their start and end apart: 48, of which 36 were waited for; matrix products, arithmetic and copies ran while one was open for 12% of the time, Pallas kernels for 0%

profile of v1, /device:TPU:8, one launch (start us, length us, event | category | flops | bytes accessed | tf_op | source)
XLA Modules:
  0.0 803.2 jit_solution(15779343162226646467)
XLA Ops:
  18.8 9.1 %all-to-all-done.1 = bf16[64,16,384]{2,0,1:T(8,128)(2,1)} async-done(((bf16[64,16,384]{2,0,1:T(8,128)(2,1)}), bf16[64,16,384]{2,0,1:T(8,128)(2,1)}, u32[]{:S(2)}, u32[]{:S(2)}) %all-to-all-start.1) | async-done | bytes 786464 | tf_op jit(solution)/shard_map/all_to_all | solution.py:144
  27.9 7.4 all-to-all-start
  84.4 12.2 %collective-permute-done.1 = bf16[1024,128]{1,0:T(8,128)(2,1)S(1)} collective-permute-done((bf16[1024,128]{1,0:T(8,128)(2,1)S(1)}, bf16[1024,128]{1,0:T(8,128)(2,1)S(1)}, u32[]{:S(2)}, u32[]{:S(2)}) %collective-permute-start.1) | collective-permute-done | bytes 262176 | tf_op jit(solution)/shard_map/ppermute | solution.py:32
  117.8 7.9 collective-permute-done.2
  125.7 19.7 %collective-permute-done.8 = bf16[1024,128]{1,0:T(8,128)(2,1)S(1)} collective-permute-done((bf16[1024,128]{1,0:T(8,128)(2,1)S(1)}, bf16[1024,128]{1,0:T(8,128)(2,1)S(1)}, u32[]{:S(2)}, u32[]{:S(2)}) %collective-permute-start.8) | collective-permute-done | bytes 262176 | tf_op jit(solution)/shard_map/ppermute | solution.py:32
  145.4 6.5 collective-permute-done.5
  239.1 10.8 %collective-permute-done.26 = bf16[1024,128]{1,0:T(8,128)(2,1)S(1)} collective-permute-done((bf16[1024,128]{1,0:T(8,128)(2,1)S(1)}, bf16[1024,128]{1,0:T(8,128)(2,1)S(1)}, u32[]{:S(2)}, u32[]{:S(2)}) %collective-permute-start.26) | collective-permute-done | bytes 262176 | tf_op jit(solution)/shard_map/ppermute | solution.py:38
  258.6 10.3 %collective-permute-done.30 = bf16[1024,128]{1,0:T(8,128)(2,1)S(1)} collective-permute-done((bf16[1024,128]{1,0:T(8,128)(2,1)S(1)}, bf16[1024,128]{1,0:T(8,128)(2,1)S(1)}, u32[]{:S(2)}, u32[]{:S(2)}) %collective-permute-start.30) | collective-permute-done | bytes 262176 | tf_op jit(solution)/shard_map/ppermute | solution.py:38
  277.6 9.4 %collective-permute-done.34 = bf16[1024,128]{1,0:T(8,128)(2,1)S(1)} collective-permute-done((bf16[1024,128]{1,0:T(8,128)(2,1)S(1)}, bf16[1024,128]{1,0:T(8,128)(2,1)S(1)}, u32[]{:S(2)}, u32[]{:S(2)}) %collective-permute-start.34) | collective-permute-done | bytes 262176 | tf_op jit(solution)/shard_map/ppermute | solution.py:38
  295.5 11.1 %collective-permute-done.37 = bf16[512,384]{0,1:T(8,128)(2,1)S(1)} collective-permute-done((bf16[512,384]{0,1:T(8,128)(2,1)S(1)}, bf16[512,384]{0,1:T(8,128)(2,1)S(1)}, u32[]{:S(2)}, u32[]{:S(2)}) %collective-permute-start.37) | collective-permute-done | bytes 393248 | tf_op jit(solution)/shard_map/ppermute | solution.py:32
  306.7 9.3 %collective-permute-done.38 = bf16[512,384]{0,1:T(8,128)(2,1)S(1)} collective-permute-done((bf16[512,384]{0,1:T(8,128)(2,1)S(1)}, bf16[512,384]{0,1:T(8,128)(2,1)S(1)}, u32[]{:S(2)}, u32[]{:S(2)}) %collective-permute-start.38) | collective-permute-done | bytes 393248 | tf_op jit(solution)/shard_map/ppermute | solution.py:32
  329.8 7.3 stack.11
  344.6 167.6 %all-to-all-done.2 = bf16[16,1024,384]{2,1,0:T(8,128)(2,1)} async-done(((bf16[16,1024,384]{2,1,0:T(8,128)(2,1)}), bf16[16,1024,384]{2,1,0:T(8,128)(2,1)}, u32[]{:S(2)}, u32[]{:S(2)}) %all-to-all-start.2) | async-done | bytes 12582944 | tf_op jit(solution)/shard_map/all_to_all | solution.py:232
  512.1 9.7 %fusion.551 = (bf16[1,1024,384]{2,1,0:T(8,128)(2,1)}, bf16[1,1024,384]{2,1,0:T(8,128)(2,1)}, bf16[1,1024,384]{2,1,0:T(8,128)(2,1)}, bf16[1,1024,384]{2,1,0:T(8,1...) fusion(bf16[16,1024,384]{2,1,0:T(8,128)(2,1)} %all-to-all-done.2), kind=kLoop, calls=%fused_computation.725 | loop fusion | bytes 25165824 | tf_op jit(solution)/shard_map/slice | solution.py:241
  561.5 16.6 %all-to-all-done.3 = bf16[16,128,384]{2,1,0:T(8,128)(2,1)} async-done(((bf16[16,128,384]{2,1,0:T(8,128)(2,1)}), bf16[16,128,384]{2,1,0:T(8,128)(2,1)}, u32[]{:S(2)}, u32[]{:S(2)}) %all-to-all-start.3) | async-done | bytes 1572896 | tf_op jit(solution)/shard_map/all_to_all | solution.py:250
  591.6 10.8 %gather_fusion = bf16[528,3072]{1,0:T(8,128)(2,1)} fusion(bf16[256,3072]{1,0:T(8,128)(2,1)} %reshape.773, s32[1024]{0:T(1024)S(1)} %pad_clamp_fusion.1), kind=kCustom, calls=%fused_computation | custom fusion | bytes 6490176 | tf_op jit(solution)/shard_map/jit(_take)/gather | solution.py:277
  608.8 49.0 %all_to_all.58 = bf16[16,33,3072]{2,1,0:T(8,128)(2,1)} all-to-all(bf16[16,33,3072]{2,1,0:T(8,128)(2,1)S(1)} %select_multiply_fusion), channel_id=1, replica_groups=mesh['seq'=8,'exp'=16] {'exp'}, dimensions={0} | all-to-all | bytes 6488064 | tf_op jit(solution)/shard_map/all_to_all | solution.py:281
  661.6 6.6 fusion.554
  694.1 6.9 all-to-all-start.5
  703.6 50.5 %all-to-all-done.5 = bf16[16,33,3072]{2,1,0:T(8,128)(2,1)} async-done(((bf16[16,33,3072]{2,1,0:T(8,128)(2,1)}), bf16[16,33,3072]{2,1,0:T(8,128)(2,1)}, u32[]{:S(2)}, u32[]{:S(2)}) %all-to-all-start.5) | async-done | bytes 3244064 | tf_op jit(solution)/shard_map/all_to_all | solution.py:300
  758.0 9.4 %gather_fusion.1 = bf16[512,3072]{1,0:T(8,128)(2,1)} fusion(bf16[528,3072]{1,0:T(8,128)(2,1)} %reshape.776, s32[1024]{0:T(1024)S(1)} %pad_clamp_fusion), kind=kCustom, calls=%fused_computation.1 | custom fusion | bytes 6293504 | tf_op jit(solution)/shard_map/jit(_take)/gather | solution.py:312
  767.4 7.2 reshape.788
  774.6 6.5 fusion.81
  781.1 6.6 copy.267
  (338 shorter events, 319.5 us)
Async XLA Ops:
  52.1 21.5 %collective-permute-start.9 = (bf16[1024,128]{1,0:T(8,128)(2,1)S(1)}, bf16[1024,128]{1,0:T(8,128)(2,1)S(1)}, u32[]{:S(2)}, u32[]{:S(2)}) collective-permute-start(bf16[1024,128]{1,0:T(8,128)(2,1)S(1)} %get-tuple-element.58), channel_id=1, source_target_pairs={{0,16},{16,32},{32,48},{48,64},{64,80},{80,96},{96,112},{112,0},{1... | collective-permute-start | bytes 786440 | tf_op jit(solution)/shard_map/ppermute | solution.py:38
  53.6 25.6 %collective-permute-start.11 = (bf16[1024,128]{1,0:T(8,128)(2,1)S(1)}, bf16[1024,128]{1,0:T(8,128)(2,1)S(1)}, u32[]{:S(2)}, u32[]{:S(2)}) collective-permute-start(bf16[1024,128]{1,0:T(8,128)(2,1)S(1)} %get-tuple-element.55), channel_id=1, source_target_pairs={{0,16},{16,32},{32,48},{48,64},{64,80},{80,96},{96,112},{112,0},{1... | collective-permute-start | bytes 786440 | tf_op jit(solution)/shard_map/ppermute | solution.py:38
  57.8 54.8 %collective-permute-start.4 = (bf16[512,3,128]{2,0,1:T(8,128)(2,1)}, bf16[512,3,128]{2,0,1:T(8,128)(2,1)S(1)}, u32[]{:S(2)}, u32[]{:S(2)}) collective-permute-start(bf16[512,3,128]{2,0,1:T(8,128)(2,1)} %collective-permute-done.3), channel_id=1, source_target_pairs={{0,32},{16,48},{32,0},{48,16},{64,96},{80,112},{96,64},{112,80},{1... | collective-permute-start | bytes 1179656 | tf_op jit(solution)/shard_map/ppermute | solution.py:32
  63.4 33.2 %collective-permute-start.1 = (bf16[1024,128]{1,0:T(8,128)(2,1)S(1)}, bf16[1024,128]{1,0:T(8,128)(2,1)S(1)}, u32[]{:S(2)}, u32[]{:S(2)}) collective-permute-start(bf16[1024,128]{1,0:T(8,128)(2,1)S(1)} %collective-permute-done), channel_id=1, source_target_pairs={{0,32},{16,48},{32,0},{48,16},{64,96},{80,112},{96,64},{112,80},{1... | collective-permute-start | bytes 786440 | tf_op jit(solution)/shard_map/ppermute | solution.py:32
  69.0 33.1 %collective-permute-start.7 = (bf16[1024,128]{1,0:T(8,128)(2,1)S(1)}, bf16[1024,128]{1,0:T(8,128)(2,1)S(1)}, u32[]{:S(2)}, u32[]{:S(2)}) collective-permute-start(bf16[1024,128]{1,0:T(8,128)(2,1)S(1)} %collective-permute-done.6), channel_id=1, source_target_pairs={{0,32},{16,48},{32,0},{48,16},{64,96},{80,112},{96,64},{112,80},{1... | collective-permute-start | bytes 786440 | tf_op jit(solution)/shard_map/ppermute | solution.py:32
  73.6 32.2 %collective-permute-start.13 = (bf16[1024,128]{1,0:T(8,128)(2,1)S(1)}, bf16[1024,128]{1,0:T(8,128)(2,1)S(1)}, u32[]{:S(2)}, u32[]{:S(2)}) collective-permute-start(bf16[1024,128]{1,0:T(8,128)(2,1)S(1)} %collective-permute-done.9), channel_id=1, source_target_pairs={{0,16},{16,32},{32,48},{48,64},{64,80},{80,96},{96,112},{112,0},{1... | collective-permute-start | bytes 786440 | tf_op jit(solution)/shard_map/ppermute | solution.py:38
  79.2 31.4 %collective-permute-start.15 = (bf16[1024,128]{1,0:T(8,128)(2,1)S(1)}, bf16[1024,128]{1,0:T(8,128)(2,1)S(1)}, u32[]{:S(2)}, u32[]{:S(2)}) collective-permute-start(bf16[1024,128]{1,0:T(8,128)(2,1)S(1)} %collective-permute-done.11), channel_id=1, source_target_pairs={{0,16},{16,32},{32,48},{48,64},{64,80},{80,96},{96,112},{112,0},{1... | collective-permute-start | bytes 786440 | tf_op jit(solution)/shard_map/ppermute | solution.py:38
  96.6 29.1 %collective-permute-start.2 = (bf16[1024,128]{1,0:T(8,128)(2,1)S(1)}, bf16[1024,128]{1,0:T(8,128)(2,1)S(1)}, u32[]{:S(2)}, u32[]{:S(2)}) collective-permute-start(bf16[1024,128]{1,0:T(8,128)(2,1)S(1)} %collective-permute-done.1), channel_id=1, source_target_pairs={{0,64},{16,80},{32,96},{48,112},{64,0},{80,16},{96,32},{112,48},{1... | collective-permute-start | bytes 786440 | tf_op jit(solution)/shard_map/ppermute | solution.py:32
  102.1 43.2 %collective-permute-start.8 = (bf16[1024,128]{1,0:T(8,128)(2,1)S(1)}, bf16[1024,128]{1,0:T(8,128)(2,1)S(1)}, u32[]{:S(2)}, u32[]{:S(2)}) collective-permute-start(bf16[1024,128]{1,0:T(8,128)(2,1)S(1)} %collective-permute-done.7), channel_id=1, source_target_pairs={{0,64},{16,80},{32,96},{48,112},{64,0},{80,16},{96,32},{112,48},{1... | collective-permute-start | bytes 786440 | tf_op jit(solution)/shard_map/ppermute | solution.py:32
  105.8 39.6 %collective-permute-start.17 = (bf16[1024,128]{1,0:T(8,128)(2,1)S(1)}, bf16[1024,128]{1,0:T(8,128)(2,1)S(1)}, u32[]{:S(2)}, u32[]{:S(2)}) collective-permute-start(bf16[1024,128]{1,0:T(8,128)(2,1)S(1)} %collective-permute-done.13), channel_id=1, source_target_pairs={{0,16},{16,32},{32,48},{48,64},{64,80},{80,96},{96,112},{112,0},{1... | collective-permute-start | bytes 786440 | tf_op jit(solution)/shard_map/ppermute | solution.py:38
  110.6 34.7 %collective-permute-start.19 = (bf16[1024,128]{1,0:T(8,128)(2,1)S(1)}, bf16[1024,128]{1,0:T(8,128)(2,1)S(1)}, u32[]{:S(2)}, u32[]{:S(2)}) collective-permute-start(bf16[1024,128]{1,0:T(8,128)(2,1)S(1)} %collective-permute-done.15), channel_id=1, source_target_pairs={{0,16},{16,32},{32,48},{48,64},{64,80},{80,96},{96,112},{112,0},{1... | collective-permute-start | bytes 786440 | tf_op jit(solution)/shard_map/ppermute | solution.py:38
  112.7 39.3 %collective-permute-start.5 = (bf16[512,3,128]{2,0,1:T(8,128)(2,1)S(1)}, bf16[512,3,128]{2,0,1:T(8,128)(2,1)S(1)}, u32[]{:S(2)}, u32[]{:S(2)}) collective-permute-start(bf16[512,3,128]{2,0,1:T(8,128)(2,1)S(1)} %collective-permute-done.4), channel_id=1, source_target_pairs={{0,64},{16,80},{32,96},{48,112},{64,0},{80,16},{96,32},{112,48},{1... | collective-permute-start | bytes 1179656 | tf_op jit(solution)/shard_map/ppermute | solution.py:32
  125.7 37.5 %collective-permute-start.10 = (bf16[1024,128]{1,0:T(8,128)(2,1)S(1)}, bf16[1024,128]{1,0:T(8,128)(2,1)S(1)}, u32[]{:S(2)}, u32[]{:S(2)}) collective-permute-start(bf16[1024,128]{1,0:T(8,128)(2,1)S(1)} %collective-permute-done.2), channel_id=1, source_target_pairs={{0,16},{16,32},{32,48},{48,64},{64,80},{80,96},{96,112},{112,0},{1... | collective-permute-start | bytes 786440 | tf_op jit(solution)/shard_map/ppermute | solution.py:38
  145.3 27.4 %collective-permute-start.21 = (bf16[1024,128]{1,0:T(8,128)(2,1)S(1)}, bf16[1024,128]{1,0:T(8,128)(2,1)S(1)}, u32[]{:S(2)}, u32[]{:S(2)}) collective-permute-start(bf16[1024,128]{1,0:T(8,128)(2,1)S(1)} %collective-permute-done.17), channel_id=1, source_target_pairs={{0,16},{16,32},{32,48},{48,64},{64,80},{80,96},{96,112},{112,0},{1... | collective-permute-start | bytes 786440 | tf_op jit(solution)/shard_map/ppermute | solution.py:38
  145.4 27.7 %collective-permute-start.23 = (bf16[1024,128]{1,0:T(8,128)(2,1)S(1)}, bf16[1024,128]{1,0:T(8,128)(2,1)S(1)}, u32[]{:S(2)}, u32[]{:S(2)}) collective-permute-start(bf16[1024,128]{1,0:T(8,128)(2,1)S(1)} %collective-permute-done.19), channel_id=1, source_target_pairs={{0,16},{16,32},{32,48},{48,64},{64,80},{80,96},{96,112},{112,0},{1... | collective-permute-start | bytes 786440 | tf_op jit(solution)/shard_map/ppermute | solution.py:38
  173.0 26.3 %collective-permute-start.27 = (bf16[1024,128]{1,0:T(8,128)(2,1)S(1)}, bf16[1024,128]{1,0:T(8,128)(2,1)S(1)}, u32[]{:S(2)}, u32[]{:S(2)}) collective-permute-start(bf16[1024,128]{1,0:T(8,128)(2,1)S(1)} %collective-permute-done.23), channel_id=1, source_target_pairs={{0,16},{16,32},{32,48},{48,64},{64,80},{80,96},{96,112},{112,0},{1... | collective-permute-start | bytes 786440 | tf_op jit(solution)/shard_map/ppermute | solution.py:38
  193.7 22.5 %collective-permute-start.29 = (bf16[1024,128]{1,0:T(8,128)(2,1)S(1)}, bf16[1024,128]{1,0:T(8,128)(2,1)S(1)}, u32[]{:S(2)}, u32[]{:S(2)}) collective-permute-start(bf16[1024,128]{1,0:T(8,128)(2,1)S(1)} %collective-permute-done.25), channel_id=1, source_target_pairs={{0,16},{16,32},{32,48},{48,64},{64,80},{80,96},{96,112},{112,0},{1... | collective-permute-start | bytes 786440 | tf_op jit(solution)/shard_map/ppermute | solution.py:38
  199.3 22.5 %collective-permute-start.31 = (bf16[1024,128]{1,0:T(8,128)(2,1)S(1)}, bf16[1024,128]{1,0:T(8,128)(2,1)S(1)}, u32[]{:S(2)}, u32[]{:S(2)}) collective-permute-start(bf16[1024,128]{1,0:T(8,128)(2,1)S(1)} %collective-permute-done.27), channel_id=1, source_target_pairs={{0,16},{16,32},{32,48},{48,64},{64,80},{80,96},{96,112},{112,0},{1... | collective-permute-start | bytes 786440 | tf_op jit(solution)/shard_map/ppermute | solution.py:38
  216.2 61.4 %collective-permute-start.33 = (bf16[1024,128]{1,0:T(8,128)(2,1)S(1)}, bf16[1024,128]{1,0:T(8,128)(2,1)S(1)}, u32[]{:S(2)}, u32[]{:S(2)}) collective-permute-start(bf16[1024,128]{1,0:T(8,128)(2,1)S(1)} %collective-permute-done.29), channel_id=1, source_target_pairs={{0,16},{16,32},{32,48},{48,64},{64,80},{80,96},{96,112},{112,0},{1... | collective-permute-start | bytes 786440 | tf_op jit(solution)/shard_map/ppermute | solution.py:38
  221.8 67.7 %collective-permute-start.35 = (bf16[1024,128]{1,0:T(8,128)(2,1)S(1)}, bf16[1024,128]{1,0:T(8,128)(2,1)S(1)}, u32[]{:S(2)}, u32[]{:S(2)}) collective-permute-start(bf16[1024,128]{1,0:T(8,128)(2,1)S(1)} %collective-permute-done.31), channel_id=1, source_target_pairs={{0,16},{16,32},{32,48},{48,64},{64,80},{80,96},{96,112},{112,0},{1... | collective-permute-start | bytes 786440 | tf_op jit(solution)/shard_map/ppermute | solution.py:38
  337.1 175.1 %all-to-all-start.2 = ((bf16[16,1024,384]{2,1,0:T(8,128)(2,1)}), bf16[16,1024,384]{2,1,0:T(8,128)(2,1)}, u32[]{:S(2)}, u32[]{:S(2)}) async-start(bf16[16,1024,384]{2,1,0:T(8,128)(2,1)} %stack.11), calls=%async_computation.2 | async-start | bytes 25165824 | tf_op jit(solution)/shard_map/all_to_all | solution.py:232
  342.8 179.2 %all-gather.2.cloned.1.call-start = ((), (), s32[]{:S(2)}) async-start(), calls=%async_computation.6 | async-start | bytes 2654208 | tf_op jit(solution)/shard_map/all_gather | solution.py:227
  552.4 25.7 %all-to-all-start.3 = ((bf16[16,128,384]{2,1,0:T(8,128)(2,1)}), bf16[16,128,384]{2,1,0:T(8,128)(2,1)}, u32[]{:S(2)}, u32[]{:S(2)}) async-start(bf16[16,128,384]{2,1,0:T(8,128)(2,1)} %copy.257), calls=%async_computation.3 | async-start | bytes 3145728 | tf_op jit(solution)/shard_map/all_to_all | solution.py:250
  694.1 60.1 %all-to-all-start.5 = ((bf16[16,33,3072]{2,1,0:T(8,128)(2,1)}), bf16[16,33,3072]{2,1,0:T(8,128)(2,1)}, u32[]{:S(2)}, u32[]{:S(2)}) async-start(bf16[16,33,3072]{2,1,0:T(8,128)(2,1)} %reshape.775), calls=%async_computation.5 | async-start | bytes 7864320 | tf_op jit(solution)/shard_map/all_to_all | solution.py:300
  (50 other events, 1184.4 us)
Sparse Core Ops, SparseCore 0:
  345.9 159.4 all-gather.1
